TPU v7x, 256 devices: a whole 4x4x8 slice. The times are simulated.
256 devices in a mesh: branch: 2 (over z_lo), batch: 32 (over y, z_hi, core), rows: 4 (over x).
Axes of the slice: x: 4, y: 4, z: 8 (z_hi: 4, z_lo: 2; z = z_hi * 2 + z_lo), core: 2. Of those that a mesh axis runs over, the one named last changes fastest.
Arguments:
- timestep: int32 [32], P('batch'), parts along dimension 0, may hold values from 0 to 999
- features: bfloat16 [32, 2, 32, 64, 640], P('batch', 'branch', 'rows'), parts along dimension 0, may hold values from -6 to 6
- conv1_weight: bfloat16 [2, 3, 3, 640, 640], P('branch', None, None, None, 'rows'), may hold values from -0.078125 to 0.078125
- conv1_bias: float32 [2, 640], P('branch'), may hold values from -3 to 3
- conv2_weight: bfloat16 [2, 3, 3, 640, 640], P('branch', None, None, None, 'rows'), may hold values from -0.078125 to 0.078125
- conv2_bias: float32 [2, 640], P('branch'), may hold values from -3 to 3
- norm1_gain: float32 [2, 640], P('branch'), may hold values from 0.25 to 1.75
- norm1_shift: float32 [2, 640], P('branch'), may hold values from -3 to 3
- norm2_gain: float32 [2, 640], P('branch'), may hold values from 0.25 to 1.75
- norm2_shift: float32 [2, 640], P('branch'), may hold values from -3 to 3
- time_weight: bfloat16 [2, 320, 1280], P('branch'), may hold values from -0.3125 to 0.3125
- emb_weight: bfloat16 [2, 1280, 640], P('branch'), may hold values from -0.15625 to 0.15625
- zero_weight: bfloat16 [640, 640], replicated, may hold values from -0.25 to 0.25
- zero_bias: float32 [640], replicated, may hold values from -3 to 3
Outputs:
- block_out: bfloat16 [32, 2, 32, 64, 640], P('batch', 'branch', 'rows'), parts along dimension 0
There are 32 independent parts, one for each index of `batch`. A program takes and returns all parts, laid end to end along the dimension named above; an argument that names none is the same for every part. Nothing has to cross between parts.
All inputs are finite; a program needn't handle non-finite values.
Results may differ from a plain program's by a relative error of at most 0.01.
Values may be sent and summed in bfloat16 or wider, within the bound.
A program may use at most 128 MiB of HBM per device.

v0:
```python
import math
import jax
import jax.numpy as jnp
from jax import lax
from jax.sharding import PartitionSpec as P

GROUPS = 32


def from_everyone(x, axis):
    copies = jnp.broadcast_to(x, (lax.axis_size(axis), *x.shape))
    return lax.all_to_all(copies, axis, split_axis=0, concat_axis=0, tiled=True)


def laid_out(pieces, dim):
    pieces = jnp.moveaxis(pieces, 0, dim)
    dims = pieces.shape
    return pieces.reshape(*dims[:dim], dims[dim] * dims[dim + 1], *dims[dim + 2 :])


def gathered_copies(x, axis, dim):
    pieces = from_everyone(x, axis)
    return laid_out(pieces, dim)


def as_sent(x):

    def short(part):
        return part.astype(jnp.bfloat16) if part.dtype == jnp.float32 else part

    return jax.tree.map(short, x)


def from_behind(x, axis, by):
    length = lax.axis_size(axis)
    pairs = [(i, i + by) for i in range(length) if 0 <= i + by < length]
    return lax.ppermute(x, axis, pairs)


def sinusoid(timestep, count):
    half = count // 2
    freqs = jnp.exp(-math.log(10000.0) * jnp.arange(half, dtype=jnp.float32) / half)
    angles = timestep.astype(jnp.float32)[0] * freqs
    return jnp.concatenate([jnp.cos(angles), jnp.sin(angles)])


def time_shift(timestep, time_weight, emb_weight):
    waves = sinusoid(timestep, time_weight.shape[0])
    inner = jax.nn.silu(jnp.dot(waves, time_weight.astype(jnp.float32)))
    return jnp.dot(inner, emb_weight.astype(jnp.float32))


def group_sums(values, groups):
    rows, cols, chans = values.shape
    grouped = values.reshape(rows, cols, groups, chans // groups)
    return (jnp.sum(grouped, axis=(0, 1, 3)), jnp.sum(grouped * grouped, axis=(0, 1, 3)))


def apply_norm(values, total, square, count, gain, shift):
    rows, cols, chans = values.shape
    groups = total.shape[0]
    mean = total / count
    var = square / count - mean * mean
    grouped = values.reshape(rows, cols, groups, chans // groups)
    normed = (grouped - mean[:, None]) * lax.rsqrt(var + 1e-05)[:, None]
    return jax.nn.silu(normed.reshape(values.shape) * gain + shift).astype(jnp.bfloat16)


def convolve(inputs, kernel, padding):
    return lax.conv_general_dilated(
        inputs[None],
        kernel,
        (1, 1),
        padding,
        dimension_numbers=("NHWC", "HWIO", "NHWC"),
        preferred_element_type=jnp.float32,
    )[0]


def body(
    timestep,
    features,
    conv1_weight,
    conv1_bias,
    conv2_weight,
    conv2_bias,
    norm1_gain,
    norm1_shift,
    norm2_gain,
    norm2_shift,
    time_weight,
    emb_weight,
    zero_weight,
    zero_bias,
):
    inputs = features[0, 0]
    rows_here, width, chans = inputs.shape
    parts = lax.axis_size("rows")
    full = rows_here * parts
    per_group = chans // GROUPS
    count = full * width * per_group
    extra = time_shift(timestep, time_weight[0], emb_weight[0])
    quarter = conv1_weight.shape[4]
    first = lax.axis_index("rows") * quarter

    def mine(vector):
        return lax.dynamic_slice_in_dim(vector, first, quarter, 0)

    all_rows = gathered_copies(inputs, "rows", 0)
    wide = all_rows.astype(jnp.float32)
    total, square = group_sums(wide, GROUPS)
    act = apply_norm(wide, total, square, count, norm1_gain[0], norm1_shift[0])
    hidden = (convolve(act, conv1_weight[0], "SAME") + mine(conv1_bias[0]) + mine(extra)).astype(
        jnp.bfloat16
    )
    hidden_wide = hidden.astype(jnp.float32)
    total, square = group_sums(hidden_wide, quarter // per_group)
    act_two = apply_norm(
        hidden_wide, total, square, count, mine(norm2_gain[0]), mine(norm2_shift[0])
    )
    piece = gathered_copies(act_two, "rows", 2)
    kernel = lax.slice_in_dim(conv2_weight[0], 0, piece.shape[2], axis=2)
    summed = jnp.zeros((full, width, quarter), jnp.float32) + convolve(piece, kernel, "SAME")
    own_part = lax.dynamic_slice_in_dim(wide, first, quarter, 2)
    partial_block = own_part + summed + mine(conv2_bias[0])
    block = lax.all_to_all(
        as_sent(partial_block), "rows", split_axis=0, concat_axis=2, tiled=True
    ).astype(partial_block.dtype)
    own_out = block.astype(jnp.bfloat16)
    flat = own_out.reshape(-1, chans)
    control = (jnp.dot(flat, zero_weight, preferred_element_type=jnp.float32) + zero_bias).astype(
        jnp.bfloat16
    )
    arrived = from_behind(control.reshape(own_out.shape), "branch", 1)
    result = (block + arrived.astype(jnp.float32)).astype(jnp.bfloat16)
    return result[None, None]


def solution(mesh):
    placed = (
        P("batch"),
        P("batch", "branch", "rows", None, None),
        P("branch", None, None, None, "rows"),
        P("branch", None),
        P("branch", None, None, None, "rows"),
        P("branch", None),
        P("branch", None),
        P("branch", None),
        P("branch", None),
        P("branch", None),
        P("branch", None, None),
        P("branch", None, None),
        P(),
        P(),
    )
    return jax.shard_map(
        body,
        mesh=mesh,
        in_specs=placed,
        out_specs=P("batch", "branch", "rows", None, None),
        check_vma=False,
    )
```

profile of v0, /device:TPU:176, one launch (start us, length us, event | category | flops | bytes accessed | tf_op | source)
XLA Modules:
  0.0 200.0 jit_solution(5692599399322577108)
XLA Ops:
  0.0 1.6 copy.52
  1.6 1.7 broadcast_in_dim.6
  3.3 4.7 %all-to-all-start = ((bf16[4,8,64,640]{3,1,2,0:T(8,128)(2,1)}), bf16[4,8,64,640]{3,1,2,0:T(8,128)(2,1)}, u32[]{:S(2)}, u32[]{:S(2)}) async-start(bf16[4,8,64,640]{3,1,2,0:T(8,128)(2,1)} %broadcast_in_dim.6), calls=%async_computation | async-start | bytes 5242880 | tf_op jit(solution)/shard_map/all_to_all | solution.py:12
  8.8 1.4 convolution_reduce_fusion
  10.7 0.8 constant_dynamic-slice_fusion.3
  11.5 0.8 constant_dynamic-slice_fusion.1
  12.2 28.1 %all-to-all-done = bf16[4,8,64,640]{3,1,2,0:T(8,128)(2,1)} async-done(((bf16[4,8,64,640]{3,1,2,0:T(8,128)(2,1)}), bf16[4,8,64,640]{3,1,2,0:T(8,128)(2,1)}, u32[]{:S(2)}, u32[]{:S(2)}) %all-to-all-start) | async-done | bytes 2621472 | tf_op jit(solution)/shard_map/all_to_all | solution.py:12
  40.3 2.5 %convert_reduce_fusion = (f32[640]{0:T(1024)S(1)}, f32[640]{0:T(1024)S(1)}) fusion(bf16[4,8,64,640]{3,1,2,0:T(8,128)(2,1)} %all-to-all-done), kind=kLoop, calls=%fused_computation.24 | loop fusion | flops 5241600 | bytes 2626560 | tf_op jit(solution)/shard_map/reduce_sum | solution.py:56
  43.6 3.6 %fusion.19 = bf16[32,1,64,640]{3,0,2,1:T(8,128)(2,1)S(1)} fusion(f32[640]{0:T(1024)S(1)} %reduce.9, f32[640]{0:T(1024)S(1)} %reduce.8, f32[640]{0:T(1024)S(1)} %mul.116, f32[640]{0:T(1024)S(1)} %sub.48, bf16[4,8,64,640]{3,1,2,0:T(8,128)(2,1)} %all-to-all-done), kind=kLoop, calls=%fused_computation.25 | loop fusion | flops 13107200 | bytes 5253120 | tf_op jit(solution)/shard_map/convert_element_type | solution.py:66
  47.4 1.0 copy.56
  48.6 9.4 %fusion.20 = (f32[160]{0:T(256)S(1)}, f32[160]{0:T(256)S(1)}, f32[32,8,9,160]{3,1,2,0:T(8,128)}) fusion(pred[8,9]{0,1:T(8,128)(4,1)S(1)} %copy-done.7, f32[160]{0:T(256)S(1)} %dynamic_slice.20, f32[160]{0:T(256)S(1)} %bitcast.96, bf16[1,3,3,640,160]{3,4,2,1,0:T(8,128)(2,1)S(1)} %copy-done, bf16[32,1,7,2,640]{4,2,3,0,1:T(8,128)(2,1)S(1)} %slice.4, ...), kind=kOutput, calls=%fused_computation.26 | convolution fusion | flops 4172758528 | bytes 6842952 | tf_op jit(solution)/shard_map/conv_general_dilated | solution.py:70
  58.8 2.4 %copy.57 = f32[32,8,9,160]{3,0,2,1:T(8,128)S(1)} copy(f32[32,8,9,160]{3,1,2,0:T(8,128)} %get-tuple-element.13) | data formatting | bytes 2949120 | tf_op jit(solution)/shard_map/conv_general_dilated | solution.py:70
  61.2 0.8 multiply_convert_fusion.1
  62.6 14.3 %broadcast_in_dim.7 = bf16[4,32,64,160]{3,2,1,0:T(8,128)(2,1)} broadcast(bf16[32,64,160]{2,1,0:T(8,128)(2,1)S(1)} %copy.58), dimensions={1,2,3} | broadcast | bytes 3276800 | tf_op jit(solution)/shard_map/broadcast_in_dim | solution.py:11
  76.9 4.9 %all-to-all-start.1 = ((bf16[4,32,64,160]{3,2,1,0:T(8,128)(2,1)}), bf16[4,32,64,160]{3,2,1,0:T(8,128)(2,1)}, u32[]{:S(2)}, u32[]{:S(2)}) async-start(bf16[4,32,64,160]{3,2,1,0:T(8,128)(2,1)} %broadcast_in_dim.7), calls=%async_computation.1 | async-start | bytes 8388608 | tf_op jit(solution)/shard_map/all_to_all | solution.py:12
  81.8 0.8 constant_dynamic-slice_fusion
  82.6 4.7 %copy_bitcast_fusion = f32[32,64,640]{2,0,1:T(8,128)} fusion(bf16[4,8,64,640]{3,1,2,0:T(8,128)(2,1)} %all-to-all-done), kind=kLoop, calls=%fused_computation.9 | loop fusion | flops 1310720 | bytes 7864320 | tf_op jit(solution)/shard_map/convert_element_type | solution.py:110
  87.3 42.8 %all-to-all-done.1 = bf16[4,32,64,160]{3,2,1,0:T(8,128)(2,1)} async-done(((bf16[4,32,64,160]{3,2,1,0:T(8,128)(2,1)}), bf16[4,32,64,160]{3,2,1,0:T(8,128)(2,1)}, u32[]{:S(2)}, u32[]{:S(2)}) %all-to-all-start.1) | async-done | bytes 2621472 | tf_op jit(solution)/shard_map/all_to_all | solution.py:12
  130.1 7.5 %copy.68 = bf16[32,64,4,160]{3,2,0,1:T(4,128)(2,1)} copy(bf16[32,64,4,160]{3,1,0,2:T(8,128)(2,1)} %bitcast.15) | data formatting | bytes 5242880
  137.6 7.9 %reshape.170 = bf16[32,1,64,640]{3,0,2,1:T(8,128)(2,1)} reshape(bf16[32,64,4,160]{3,2,0,1:T(4,128)(2,1)} %copy.68) | data formatting | bytes 5242880
  145.5 2.0 pad.2.clone
  147.5 1.0 copy.62
  148.9 8.4 %fusion.35 = f32[32,8,9,160]{3,1,2,0:T(8,128)S(1)} fusion(bf16[1,3,3,640,160]{3,4,2,1,0:T(8,128)(2,1)S(1)} %copy-done.5, bf16[32,1,7,2,640]{4,2,3,0,1:T(8,128)(2,1)S(1)} %slice.6, bf16[32,1,8,9,640]{4,2,3,0,1:T(8,128)(2,1)S(1)} %copy.62, pred[8,9]{0,1:T(8,128)(4,1)S(1)} %copy-done.7), kind=kOutput, calls=%fused_computation.45 | convolution fusion | flops 4169441280 | bytes 6840392 | tf_op jit(solution)/shard_map/conv_general_dilated | solution.py:70
  158.1 2.6 %fusion.25 = bf16[32,64,160]{2,0,1:T(8,128)(2,1)S(1)} fusion(f32[32,1,72,160]{3,0,2,1:T(8,128)S(1)} %bitcast.94, f32[32,64,640]{2,0,1:T(8,128)} %copy_bitcast_fusion, s32[]{:T(128)S(6)} %select_n.2, f32[160]{0:T(256)S(1)} %bitcast.98), kind=kLoop, calls=%fused_computation.33 | loop fusion | flops 983040 | bytes 3277444 | tf_op jit(solution)/shard_map/convert_element_type | solution.py:29
  161.3 16.1 %all_to_all.25 = bf16[32,64,160]{2,1,0:T(8,128)(2,1)S(1)} all-to-all(bf16[32,64,160]{2,1,0:T(8,128)(2,1)S(1)} %copy.64), channel_id=1, replica_groups=mesh['branch'=2,'batch'=32,'rows'=4] {'rows'}, dimensions={0} | all-to-all | bytes 1310720 | tf_op jit(solution)/shard_map/all_to_all | solution.py:126
  177.4 0.8 copy.66
  178.9 2.7 %fusion.45 = bf16[512,640]{1,0:T(8,128)(2,1)} fusion(bf16[512,640]{1,0:T(8,128)(2,1)S(1)} %reshape.128, bf16[640,640]{1,0:T(8,128)(2,1)} %param.26, f32[640]{0:T(1024)S(1)} %copy-done.6), kind=kOutput, calls=%fused_computation.48 | convolution fusion | flops 420085760 | bytes 2132480 | tf_op jit(solution)/shard_map/dot_general | solution.py:131
  181.6 1.3 collective-permute-start
  182.9 2.2 %copy.65 = f32[8,64,4,160]{3,2,1,0:T(4,128)} copy(bf16[8,64,4,160]{3,1,0,2:T(8,128)(2,1)S(1)} %bitcast.92) | data formatting | bytes 1966080 | tf_op jit(solution)/shard_map/convert_element_type | solution.py:128
  185.1 2.6 %reshape.148 = f32[8,64,640]{2,1,0:T(8,128)S(1)} reshape(f32[8,64,4,160]{3,2,1,0:T(4,128)} %copy.65) | data formatting | bytes 2621440 | tf_op jit(solution)/shard_map/convert_element_type | solution.py:128
  187.7 10.0 %collective-permute-done = bf16[8,64,640]{2,1,0:T(8,128)(2,1)} collective-permute-done((bf16[8,64,640]{2,1,0:T(8,128)(2,1)}, bf16[8,64,640]{2,1,0:T(8,128)(2,1)}, u32[]{:S(2)}, u32[]{:S(2)}) %collective-permute-start) | collective-permute-done | bytes 655392 | tf_op jit(solution)/shard_map/ppermute | solution.py:37
  197.7 2.1 %fusion.50 = bf16[1,1,8,64,640]{4,3,2,1,0:T(8,128)(2,1)} fusion(f32[8,64,640]{2,1,0:T(8,128)S(1)} %reshape.148, bf16[8,64,640]{2,1,0:T(8,128)(2,1)} %collective-permute-done), kind=kLoop, calls=%fused_computation.53 | loop fusion | flops 983040 | bytes 2621440 | tf_op jit(solution)/shard_map/broadcast_in_dim | solution.py:136
  (50 shorter events, 5.6 us)
Async XLA Ops:
  0.0 48.6 %copy-start = (bf16[1,3,3,640,160]{3,4,2,1,0:T(8,128)(2,1)S(1)}, bf16[1,3,3,640,160]{3,4,2,1,0:T(8,128)(2,1)}, u32[]{:S(2)}) copy-start(bf16[1,3,3,640,160]{3,4,2,1,0:T(8,128)(2,1)} %param.16) | copy-start | bytes 5529604
  3.3 4.7 %copy-start.3 = (f32[1,640]{1,0:T(1,128)S(1)}, f32[1,640]{1,0:T(1,128)}, u32[]{:S(2)}) copy-start(f32[1,640]{1,0:T(1,128)} %param.20) | copy-start | bytes 7684
  3.3 4.7 %copy-start.4 = (f32[1,640]{1,0:T(1,128)S(1)}, f32[1,640]{1,0:T(1,128)}, u32[]{:S(2)}) copy-start(f32[1,640]{1,0:T(1,128)} %param.21) | copy-start | bytes 7684
  3.3 7.0 %copy-start.2 = (bf16[1,1280,640]{2,1,0:T(8,128)(2,1)S(1)}, bf16[1,1280,640]{2,1,0:T(8,128)(2,1)}, u32[]{:S(2)}) copy-start(bf16[1,1280,640]{2,1,0:T(8,128)(2,1)} %param.25) | copy-start | bytes 4915204
  3.3 37.0 %all-to-all-start = ((bf16[4,8,64,640]{3,1,2,0:T(8,128)(2,1)}), bf16[4,8,64,640]{3,1,2,0:T(8,128)(2,1)}, u32[]{:S(2)}, u32[]{:S(2)}) async-start(bf16[4,8,64,640]{3,1,2,0:T(8,128)(2,1)} %broadcast_in_dim.6), calls=%async_computation | async-start | bytes 5242880 | tf_op jit(solution)/shard_map/all_to_all | solution.py:12
  47.4 1.2 copy-start.7
  76.9 53.2 %all-to-all-start.1 = ((bf16[4,32,64,160]{3,2,1,0:T(8,128)(2,1)}), bf16[4,32,64,160]{3,2,1,0:T(8,128)(2,1)}, u32[]{:S(2)}, u32[]{:S(2)}) async-start(bf16[4,32,64,160]{3,2,1,0:T(8,128)(2,1)} %broadcast_in_dim.7), calls=%async_computation.1 | async-start | bytes 8388608 | tf_op jit(solution)/shard_map/all_to_all | solution.py:12
  147.4 1.5 copy-start.5
  177.4 1.5 copy-start.6
  181.6 16.1 %collective-permute-start = (bf16[8,64,640]{2,1,0:T(8,128)(2,1)}, bf16[8,64,640]{2,1,0:T(8,128)(2,1)}, u32[]{:S(2)}, u32[]{:S(2)}) collective-permute-start(bf16[8,64,640]{2,1,0:T(8,128)(2,1)} %bitcast.25), channel_id=1, source_target_pairs={{0,128},{1,129},{2,130},{3,131},{4,132},{5,133},{6,134},{7,135},{8... | collective-permute-start | bytes 1966088 | tf_op jit(solution)/shard_map/ppermute | solution.py:37
  182.9 16.9 %copy-start.1 = (bf16[1,3,3,640,160]{3,4,2,1,0:T(8,128)(2,1)S(1)}, bf16[1,3,3,640,160]{3,4,2,1,0:T(8,128)(2,1)}, u32[]{:S(2)}) copy-start(bf16[1,3,3,640,160]{3,4,2,1,0:T(8,128)(2,1)} %param.16) | copy-start | bytes 5529604
where the time goes:
time: 204 us; the launch traced here: 200 us
  waiting for transfers between devices  80.9 us (40%)
  local copies, waits for them, and re-layouts  51.9 us (25%)
  matrix products  22.2 us (11%)
  other arithmetic  16.9 us (8%)
  blocking collectives  16.1 us (8%)
  starting transfers between devices  10.8 us (5%)
    all_to_all x2, waiting for transfers between devices, from_everyone(): return lax.all_to_all(copies, axis, split_axis=0, concat_axis=0, tiled=True)  70.9 us
    conv_general_dilated x2, matrix products, convolve(): lax.conv_general_dilated(inputs[None], kernel, (1, 1), padding, dimension...  17.8 us
    all_to_all x1, blocking collectives, body(): lax.all_to_all(as_sent(partial_block), 'rows', split_axis=0, concat_axis=...  16.1 us
    broadcast_in_dim x2, local copies, waits for them, and re-layouts, from_everyone(): copies = jnp.broadcast_to(x, (lax.axis_size(axis), *x.shape))  16 us
    unnamed x18, local copies, waits for them, and re-layouts  15.7 us
    ppermute x1, waiting for transfers between devices, from_behind(): return lax.ppermute(x, axis, pairs)  10 us
    all_to_all x2, starting transfers between devices, from_everyone(): return lax.all_to_all(copies, axis, split_axis=0, concat_axis=0, tiled=True)  9.55 us
    conv_general_dilated x6, local copies, waits for them, and re-layouts, convolve(): lax.conv_general_dilated(inputs[None], kernel, (1, 1), padding, dimension...  5.51 us
  transfers between devices with their start and end apart: 3, of which 3 were waited for; matrix products, arithmetic and copies ran while one was open for 7% of the time, Pallas kernels for 0%

commit v1 on v0

--- a/solution.py
+++ b/solution.py
@@ -5,6 +5,28 @@
 from jax.sharding import PartitionSpec as P
 
 GROUPS = 32
+
+
+def split_up(x, dim, size):
+    before, after = (x.shape[:dim], x.shape[dim + 1 :])
+    return jnp.moveaxis(x.reshape(*before, size, -1, *after), dim, 0)
+
+
+def joined_along(blocks, dim):
+    blocks = jnp.moveaxis(blocks, 0, dim)
+    shape = blocks.shape
+    return blocks.reshape(*shape[:dim], shape[dim] * shape[dim + 1], *shape[dim + 2 :])
+
+
+def exchange_in_pairs(array, axis, split_dim, concat_dim):
+    count, index = (lax.axis_size(axis), lax.axis_index(axis))
+    parts = split_up(array, split_dim, count)
+    outs = [parts[index]]
+    for turn in range(1, count):
+        sent = parts[index ^ turn]
+        outs.append(lax.ppermute(sent, axis, [(i, i ^ turn) for i in range(count)]))
+    parts = jnp.stack(outs)[index ^ jnp.arange(count)]
+    return joined_along(parts, concat_dim)
 
 
 def from_everyone(x, axis):
@@ -123,9 +145,7 @@
     summed = jnp.zeros((full, width, quarter), jnp.float32) + convolve(piece, kernel, "SAME")
     own_part = lax.dynamic_slice_in_dim(wide, first, quarter, 2)
     partial_block = own_part + summed + mine(conv2_bias[0])
-    block = lax.all_to_all(
-        as_sent(partial_block), "rows", split_axis=0, concat_axis=2, tiled=True
-    ).astype(partial_block.dtype)
+    block = exchange_in_pairs(as_sent(partial_block), "rows", 0, 2).astype(partial_block.dtype)
     own_out = block.astype(jnp.bfloat16)
     flat = own_out.reshape(-1, chans)
     control = (jnp.dot(flat, zero_weight, preferred_element_type=jnp.float32) + zero_bias).astype(

time: 204 us -> 205 us (level)
  blocking collectives: 16.1 us -> 0 us
  waiting for transfers between devices: 80.9 us -> 91.4 us
  starting transfers between devices: 10.8 us -> 15.6 us
    all_to_all x1 -> x0, blocking collectives: 16.1 us -> none  [body(): lax.all_to_all(as_sent(partial_block), 'rows', split_axis=0, concat_axis=...]
    ppermute x0 -> x3, waiting for transfers between devices: none -> 10.2 us  [exchange_in_pairs(): outs.append(lax.ppermute(sent, axis, [(i, i ^ turn) for i in range(count)]))]
    ppermute x0 -> x3, starting transfers between devices: none -> 4.79 us  [exchange_in_pairs(): outs.append(lax.ppermute(sent, axis, [(i, i ^ turn) for i in range(count)]))]
  transfers between devices with their start and end apart: 3 -> 6, of which waited for: 3 -> 6; matrix products, arithmetic and copies ran while one was open for 7% -> 7% of each run, Pallas kernels for 0% -> 0%
where the time goes in v1:
time: 205 us; the launch traced here: 202 us
  waiting for transfers between devices  91.4 us (45%)
  local copies, waits for them, and re-layouts  53.6 us (26%)
  matrix products  22.3 us (11%)
  other arithmetic  17.4 us (8%)
  starting transfers between devices  15.6 us (8%)
    all_to_all x2, waiting for transfers between devices, from_everyone(): return lax.all_to_all(copies, axis, split_axis=0, concat_axis=0, tiled=True)  70.8 us
    conv_general_dilated x2, matrix products, convolve(): lax.conv_general_dilated(inputs[None], kernel, (1, 1), padding, dimension...  17.8 us
    broadcast_in_dim x2, local copies, waits for them, and re-layouts, from_everyone(): copies = jnp.broadcast_to(x, (lax.axis_size(axis), *x.shape))  16.5 us
    unnamed x18, local copies, waits for them, and re-layouts  15.7 us
    ppermute x1, waiting for transfers between devices, from_behind(): return lax.ppermute(x, axis, pairs)  10.3 us
    ppermute x3, waiting for transfers between devices, exchange_in_pairs(): outs.append(lax.ppermute(sent, axis, [(i, i ^ turn) for i in range(count)]))  10.2 us
    all_to_all x2, starting transfers between devices, from_everyone(): return lax.all_to_all(copies, axis, split_axis=0, concat_axis=0, tiled=True)  9.55 us
    conv_general_dilated x6, local copies, waits for them, and re-layouts, convolve(): lax.conv_general_dilated(inputs[None], kernel, (1, 1), padding, dimension...  5.51 us
  transfers between devices with their start and end apart: 6, of which 6 were waited for; matrix products, arithmetic and copies ran while one was open for 7% of the time, Pallas kernels for 0%

profile of v1, /device:TPU:176, one launch (start us, length us, event | category | flops | bytes accessed | tf_op | source)
XLA Modules:
  0.0 201.5 jit_solution(13864157463818140079)
XLA Ops:
  0.0 1.6 copy.52
  1.6 1.7 broadcast_in_dim.6
  3.3 4.7 %all-to-all-start = ((bf16[4,8,64,640]{3,1,2,0:T(8,128)(2,1)}), bf16[4,8,64,640]{3,1,2,0:T(8,128)(2,1)}, u32[]{:S(2)}, u32[]{:S(2)}) async-start(bf16[4,8,64,640]{3,1,2,0:T(8,128)(2,1)} %broadcast_in_dim.6), calls=%async_computation | async-start | bytes 5242880 | tf_op jit(solution)/shard_map/all_to_all | solution.py:34
  8.8 1.4 convolution_reduce_fusion
  12.2 28.1 %all-to-all-done = bf16[4,8,64,640]{3,1,2,0:T(8,128)(2,1)} async-done(((bf16[4,8,64,640]{3,1,2,0:T(8,128)(2,1)}), bf16[4,8,64,640]{3,1,2,0:T(8,128)(2,1)}, u32[]{:S(2)}, u32[]{:S(2)}) %all-to-all-start) | async-done | bytes 2621472 | tf_op jit(solution)/shard_map/all_to_all | solution.py:34
  40.3 2.5 %convert_reduce_fusion = (f32[640]{0:T(1024)S(1)}, f32[640]{0:T(1024)S(1)}) fusion(bf16[4,8,64,640]{3,1,2,0:T(8,128)(2,1)} %all-to-all-done), kind=kLoop, calls=%fused_computation.25 | loop fusion | flops 5241600 | bytes 2626560 | tf_op jit(solution)/shard_map/reduce_sum | solution.py:78
  43.6 3.6 %fusion.19 = bf16[32,1,64,640]{3,0,2,1:T(8,128)(2,1)S(1)} fusion(f32[640]{0:T(1024)S(1)} %reduce.9, f32[640]{0:T(1024)S(1)} %reduce.8, f32[640]{0:T(1024)S(1)} %mul.116, f32[640]{0:T(1024)S(1)} %sub.48, bf16[4,8,64,640]{3,1,2,0:T(8,128)(2,1)} %all-to-all-done), kind=kLoop, calls=%fused_computation.26 | loop fusion | flops 13107200 | bytes 5253120 | tf_op jit(solution)/shard_map/convert_element_type | solution.py:88
  47.4 1.0 copy.56
  48.6 9.4 %fusion.20 = (f32[160]{0:T(256)S(1)}, f32[160]{0:T(256)S(1)}, f32[32,8,9,160]{3,1,2,0:T(8,128)}) fusion(pred[8,9]{0,1:T(8,128)(4,1)S(1)} %copy-done.7, f32[160]{0:T(256)S(1)} %dynamic_slice.32, f32[160]{0:T(256)S(1)} %bitcast.110, bf16[1,3,3,640,160]{3,4,2,1,0:T(8,128)(2,1)S(1)} %copy-done, bf16[32,1,7,2,640]{4,2,3,0,1:T(8,128)(2,1)S(1)} %slice.6, ...), kind=kOutput, calls=%fused_computation.27 | convolution fusion | flops 4172758528 | bytes 6842952 | tf_op jit(solution)/shard_map/conv_general_dilated | solution.py:92
  58.8 2.4 %copy.57 = f32[32,8,9,160]{3,0,2,1:T(8,128)S(1)} copy(f32[32,8,9,160]{3,1,2,0:T(8,128)} %get-tuple-element.17) | data formatting | bytes 2949120 | tf_op jit(solution)/shard_map/conv_general_dilated | solution.py:92
  62.6 14.8 %broadcast_in_dim.7 = bf16[4,32,64,160]{3,2,1,0:T(8,128)(2,1)} broadcast(bf16[32,64,160]{2,1,0:T(8,128)(2,1)S(1)} %copy.58), dimensions={1,2,3} | broadcast | bytes 3276800 | tf_op jit(solution)/shard_map/broadcast_in_dim | solution.py:33
  77.4 4.9 %all-to-all-start.1 = ((bf16[4,32,64,160]{3,2,1,0:T(8,128)(2,1)}), bf16[4,32,64,160]{3,2,1,0:T(8,128)(2,1)}, u32[]{:S(2)}, u32[]{:S(2)}) async-start(bf16[4,32,64,160]{3,2,1,0:T(8,128)(2,1)} %broadcast_in_dim.7), calls=%async_computation.1 | async-start | bytes 8388608 | tf_op jit(solution)/shard_map/all_to_all | solution.py:34
  83.1 4.7 %copy_bitcast_fusion = f32[32,64,640]{2,0,1:T(8,128)} fusion(bf16[4,8,64,640]{3,1,2,0:T(8,128)(2,1)} %all-to-all-done), kind=kLoop, calls=%fused_computation.10 | loop fusion | flops 1310720 | bytes 7864320 | tf_op jit(solution)/shard_map/convert_element_type | solution.py:132
  87.8 42.8 %all-to-all-done.1 = bf16[4,32,64,160]{3,2,1,0:T(8,128)(2,1)} async-done(((bf16[4,32,64,160]{3,2,1,0:T(8,128)(2,1)}), bf16[4,32,64,160]{3,2,1,0:T(8,128)(2,1)}, u32[]{:S(2)}, u32[]{:S(2)}) %all-to-all-start.1) | async-done | bytes 2621472 | tf_op jit(solution)/shard_map/all_to_all | solution.py:34
  130.6 7.5 %copy.68 = bf16[32,64,4,160]{3,2,0,1:T(4,128)(2,1)} copy(bf16[32,64,4,160]{3,1,0,2:T(8,128)(2,1)} %bitcast.15) | data formatting | bytes 5242880
  138.1 7.9 %reshape.199 = bf16[32,1,64,640]{3,0,2,1:T(8,128)(2,1)} reshape(bf16[32,64,4,160]{3,2,0,1:T(4,128)(2,1)} %copy.68) | data formatting | bytes 5242880
  146.0 2.0 pad.2.clone
  148.0 1.0 copy.62
  149.4 8.4 %fusion.35 = f32[32,8,9,160]{3,1,2,0:T(8,128)S(1)} fusion(bf16[1,3,3,640,160]{3,4,2,1,0:T(8,128)(2,1)S(1)} %copy-done.5, bf16[32,1,7,2,640]{4,2,3,0,1:T(8,128)(2,1)S(1)} %slice.8, bf16[32,1,8,9,640]{4,2,3,0,1:T(8,128)(2,1)S(1)} %copy.62, pred[8,9]{0,1:T(8,128)(4,1)S(1)} %copy-done.7), kind=kOutput, calls=%fused_computation.46 | convolution fusion | flops 4169441280 | bytes 6840392 | tf_op jit(solution)/shard_map/conv_general_dilated | solution.py:92
  158.6 2.6 %fusion.25 = bf16[32,64,160]{2,0,1:T(8,128)(2,1)S(1)} fusion(f32[32,1,72,160]{3,0,2,1:T(8,128)S(1)} %bitcast.104, f32[32,64,640]{2,0,1:T(8,128)} %copy_bitcast_fusion, s32[]{:T(128)S(6)} %select_n.30, f32[160]{0:T(256)S(1)} %bitcast.112), kind=kLoop, calls=%fused_computation.34 | loop fusion | flops 983040 | bytes 3277444 | tf_op jit(solution)/shard_map/convert_element_type | solution.py:51
  162.6 1.8 collective-permute-start.1
  164.3 2.4 %collective-permute-start.2 = (bf16[8,64,160]{2,1,0:T(8,128)(2,1)S(1)}, bf16[8,64,160]{2,1,0:T(8,128)(2,1)S(1)}, u32[]{:S(2)}, u32[]{:S(2)}) collective-permute-start(bf16[8,64,160]{2,1,0:T(8,128)(2,1)S(1)} %get-tuple-element.10), channel_id=1, source_target_pairs={{0,3},{1,2},{2,1},{3,0},{4,7},{5,6},{6,5},{7,4},{8,11},{9,10},{10,... | collective-permute-start | bytes 491528 | tf_op jit(solution)/shard_map/ppermute | solution.py:27
  166.7 4.4 %collective-permute-done = bf16[8,64,160]{2,1,0:T(8,128)(2,1)S(1)} collective-permute-done((bf16[8,64,160]{2,1,0:T(8,128)(2,1)S(1)}, bf16[8,64,160]{2,1,0:T(8,128)(2,1)S(1)}, u32[]{:S(2)}, u32[]{:S(2)}) %collective-permute-start) | collective-permute-done | bytes 163872 | tf_op jit(solution)/shard_map/ppermute | solution.py:27
  171.1 3.1 %collective-permute-done.1 = bf16[8,64,160]{2,1,0:T(8,128)(2,1)S(1)} collective-permute-done((bf16[8,64,160]{2,1,0:T(8,128)(2,1)S(1)}, bf16[8,64,160]{2,1,0:T(8,128)(2,1)S(1)}, u32[]{:S(2)}, u32[]{:S(2)}) %collective-permute-start.1) | collective-permute-done | bytes 163872 | tf_op jit(solution)/shard_map/ppermute | solution.py:27
  174.2 2.7 %collective-permute-done.2 = bf16[8,64,160]{2,1,0:T(8,128)(2,1)S(1)} collective-permute-done((bf16[8,64,160]{2,1,0:T(8,128)(2,1)S(1)}, bf16[8,64,160]{2,1,0:T(8,128)(2,1)S(1)}, u32[]{:S(2)}, u32[]{:S(2)}) %collective-permute-start.2) | collective-permute-done | bytes 163872 | tf_op jit(solution)/shard_map/ppermute | solution.py:27
  177.8 0.8 copy.66
  179.3 2.7 %fusion.45 = bf16[512,640]{1,0:T(8,128)(2,1)} fusion(bf16[512,640]{1,0:T(8,128)(2,1)S(1)} %reshape.149, bf16[640,640]{1,0:T(8,128)(2,1)} %param.26, f32[640]{0:T(1024)S(1)} %copy-done.6), kind=kOutput, calls=%fused_computation.49 | convolution fusion | flops 420085760 | bytes 2132480 | tf_op jit(solution)/shard_map/dot_general | solution.py:151
  182.0 1.3 collective-permute-start.3
  183.6 2.7 %copy.65 = f32[8,64,4,160]{3,2,1,0:T(4,128)} copy(f32[8,64,4,160]{3,1,0,2:T(8,128)S(1)} %bitcast_convert_fusion) | data formatting | bytes 2621440 | tf_op jit(solution)/shard_map/convert_element_type | solution.py:148
  186.3 2.6 %reshape.169 = f32[8,64,640]{2,1,0:T(8,128)S(1)} reshape(f32[8,64,4,160]{3,2,1,0:T(4,128)} %copy.65) | data formatting | bytes 2621440 | tf_op jit(solution)/shard_map/convert_element_type | solution.py:148
  188.9 10.3 %collective-permute-done.3 = bf16[8,64,640]{2,1,0:T(8,128)(2,1)} collective-permute-done((bf16[8,64,640]{2,1,0:T(8,128)(2,1)}, bf16[8,64,640]{2,1,0:T(8,128)(2,1)}, u32[]{:S(2)}, u32[]{:S(2)}) %collective-permute-start.3) | collective-permute-done | bytes 655392 | tf_op jit(solution)/shard_map/ppermute | solution.py:59
  199.2 2.1 %fusion.50 = bf16[1,1,8,64,640]{4,3,2,1,0:T(8,128)(2,1)} fusion(f32[8,64,640]{2,1,0:T(8,128)S(1)} %reshape.169, bf16[8,64,640]{2,1,0:T(8,128)(2,1)} %collective-permute-done.3), kind=kLoop, calls=%fused_computation.55 | loop fusion | flops 983040 | bytes 2621440 | tf_op jit(solution)/shard_map/broadcast_in_dim | solution.py:156
  (61 shorter events, 10.5 us)
Async XLA Ops:
  0.0 48.6 %copy-start = (bf16[1,3,3,640,160]{3,4,2,1,0:T(8,128)(2,1)S(1)}, bf16[1,3,3,640,160]{3,4,2,1,0:T(8,128)(2,1)}, u32[]{:S(2)}) copy-start(bf16[1,3,3,640,160]{3,4,2,1,0:T(8,128)(2,1)} %param.16) | copy-start | bytes 5529604
  3.3 6.9 %copy-start.3 = (f32[1,640]{1,0:T(1,128)S(1)}, f32[1,640]{1,0:T(1,128)}, u32[]{:S(2)}) copy-start(f32[1,640]{1,0:T(1,128)} %param.20) | copy-start | bytes 7684
  3.3 6.9 %copy-start.4 = (f32[1,640]{1,0:T(1,128)S(1)}, f32[1,640]{1,0:T(1,128)}, u32[]{:S(2)}) copy-start(f32[1,640]{1,0:T(1,128)} %param.21) | copy-start | bytes 7684
  3.3 7.0 %copy-start.2 = (bf16[1,1280,640]{2,1,0:T(8,128)(2,1)S(1)}, bf16[1,1280,640]{2,1,0:T(8,128)(2,1)}, u32[]{:S(2)}) copy-start(bf16[1,1280,640]{2,1,0:T(8,128)(2,1)} %param.25) | copy-start | bytes 4915204
  3.3 37.0 %all-to-all-start = ((bf16[4,8,64,640]{3,1,2,0:T(8,128)(2,1)}), bf16[4,8,64,640]{3,1,2,0:T(8,128)(2,1)}, u32[]{:S(2)}, u32[]{:S(2)}) async-start(bf16[4,8,64,640]{3,1,2,0:T(8,128)(2,1)} %broadcast_in_dim.6), calls=%async_computation | async-start | bytes 5242880 | tf_op jit(solution)/shard_map/all_to_all | solution.py:34
  47.4 1.2 copy-start.7
  77.4 53.2 %all-to-all-start.1 = ((bf16[4,32,64,160]{3,2,1,0:T(8,128)(2,1)}), bf16[4,32,64,160]{3,2,1,0:T(8,128)(2,1)}, u32[]{:S(2)}, u32[]{:S(2)}) async-start(bf16[4,32,64,160]{3,2,1,0:T(8,128)(2,1)} %broadcast_in_dim.7), calls=%async_computation.1 | async-start | bytes 8388608 | tf_op jit(solution)/shard_map/all_to_all | solution.py:34
  147.9 1.5 copy-start.5
  161.9 9.2 %collective-permute-start = (bf16[8,64,160]{2,1,0:T(8,128)(2,1)S(1)}, bf16[8,64,160]{2,1,0:T(8,128)(2,1)S(1)}, u32[]{:S(2)}, u32[]{:S(2)}) collective-permute-start(bf16[8,64,160]{2,1,0:T(8,128)(2,1)S(1)} %get-tuple-element.12), channel_id=1, source_target_pairs={{0,1},{1,0},{2,3},{3,2},{4,5},{5,4},{6,7},{7,6},{8,9},{9,8},{10,11... | collective-permute-start | bytes 491528 | tf_op jit(solution)/shard_map/ppermute | solution.py:27
  162.6 11.7 %collective-permute-start.1 = (bf16[8,64,160]{2,1,0:T(8,128)(2,1)S(1)}, bf16[8,64,160]{2,1,0:T(8,128)(2,1)S(1)}, u32[]{:S(2)}, u32[]{:S(2)}) collective-permute-start(bf16[8,64,160]{2,1,0:T(8,128)(2,1)S(1)} %get-tuple-element.11), channel_id=1, source_target_pairs={{0,2},{1,3},{2,0},{3,1},{4,6},{5,7},{6,4},{7,5},{8,10},{9,11},{10,... | collective-permute-start | bytes 491528 | tf_op jit(solution)/shard_map/ppermute | solution.py:27
  164.3 12.6 %collective-permute-start.2 = (bf16[8,64,160]{2,1,0:T(8,128)(2,1)S(1)}, bf16[8,64,160]{2,1,0:T(8,128)(2,1)S(1)}, u32[]{:S(2)}, u32[]{:S(2)}) collective-permute-start(bf16[8,64,160]{2,1,0:T(8,128)(2,1)S(1)} %get-tuple-element.10), channel_id=1, source_target_pairs={{0,3},{1,2},{2,1},{3,0},{4,7},{5,6},{6,5},{7,4},{8,11},{9,10},{10,... | collective-permute-start | bytes 491528 | tf_op jit(solution)/shard_map/ppermute | solution.py:27
  177.8 1.5 copy-start.6
  182.0 17.2 %collective-permute-start.3 = (bf16[8,64,640]{2,1,0:T(8,128)(2,1)}, bf16[8,64,640]{2,1,0:T(8,128)(2,1)}, u32[]{:S(2)}, u32[]{:S(2)}) collective-permute-start(bf16[8,64,640]{2,1,0:T(8,128)(2,1)} %bitcast.31), channel_id=1, source_target_pairs={{0,128},{1,129},{2,130},{3,131},{4,132},{5,133},{6,134},{7,135},{8... | collective-permute-start | bytes 1966088 | tf_op jit(solution)/shard_map/ppermute | solution.py:59
  183.6 17.8 %copy-start.1 = (bf16[1,3,3,640,160]{3,4,2,1,0:T(8,128)(2,1)S(1)}, bf16[1,3,3,640,160]{3,4,2,1,0:T(8,128)(2,1)}, u32[]{:S(2)}) copy-start(bf16[1,3,3,640,160]{3,4,2,1,0:T(8,128)(2,1)} %param.16) | copy-start | bytes 5529604
